TPU v7x, 32 devices: a whole 2x2x4 slice. The times are simulated.
32 devices in a mesh: tilt: 2 (over y), row: 8 (over z, x), col: 2 (over core).
Axes of the slice: x: 2, y: 2, z: 4, core: 2. Of those that a mesh axis runs over, the one named last changes fastest.
Arguments:
- object_field: float32 [2, 2048, 256], P(None, ('tilt', 'row'), 'col'), parts along dimension 1, may hold values from -4.2 to 4.2
- probe: float32 [8, 2, 128, 128], P('tilt'), parts along dimension 0, may hold values from -2.1 to 2.1
- patterns: float32 [16, 2, 2, 128, 128], P(('tilt', 'row'), 'col'), parts along dimension 0, may hold values from 0.1 to 3
- offsets: int32 [16, 2, 2, 2], P(('tilt', 'row'), 'col'), parts along dimension 0, may hold values from 0 to 256
- counts: int32 [16, 2], P(('tilt', 'row'), 'col'), parts along dimension 0, may hold values from 1 to 2, as said below
Outputs:
- object_out: float32 [2, 2048, 256], P(None, ('tilt', 'row'), 'col'), parts along dimension 1
- probe_out: float32 [8, 2, 128, 128], P('tilt'), parts along dimension 0
There are 2 independent parts, one for each index of `tilt`. A program takes and returns all parts, laid end to end along the dimension named above; each array names one. Nothing has to cross between parts.
Inputs may be any that keep to these rules, and one draw needn't show every extreme that they name: Only the first counts[r, c] slots of a tile are live; some tile has all 2 live. `offsets`: A window lies inside its tile's frame of 384 pixels a side.
All inputs are finite; a program needn't handle non-finite values.
Results may differ from a plain program's by a relative error of at most 0.0003.
Values sent between devices are 32-bit elements; how exact they have to be, the bound alone decides.
A program may use at most 64 MiB of HBM per device.

v0:
```python
import jax
import jax.numpy as jnp
from jax import lax
from jax.sharding import PartitionSpec as P

H = 128
object_rate = 1.0
probe_rate = 1.0
epsilon = 1e-06


def with_halo(block, sides, width):
    for axis, dim in sides:
        count = lax.axis_size(axis)
        forward = [(i, i + 1) for i in range(count - 1)]
        backward = [(target, source) for source, target in forward]
        low = lax.ppermute(
            lax.slice_in_dim(block, block.shape[dim] - width, None, axis=dim), axis, forward
        )
        high = lax.ppermute(lax.slice_in_dim(block, 0, width, axis=dim), axis, backward)
        block = jnp.concatenate([low, block, high], axis=dim)
    return block


def as_index(value):
    return jnp.asarray(value).astype(jnp.int32)


def dft_tables(length):
    counter = jnp.arange(length, dtype=jnp.int32)
    product = counter[:, None] * counter[None, :] % length
    angle = -2.0 * jnp.pi / length * product.astype(jnp.float32)
    norm = 1.0 / jnp.sqrt(jnp.float32(length))
    return (jnp.cos(angle) * norm, jnp.sin(angle) * norm)


def left_product(cos_table, sin_table, real_part, imag_part):
    hp = lax.Precision.HIGHEST
    real_out = jnp.einsum("ab,kbc->kac", cos_table, real_part, precision=hp) - jnp.einsum(
        "ab,kbc->kac", sin_table, imag_part, precision=hp
    )
    imag_out = jnp.einsum("ab,kbc->kac", cos_table, imag_part, precision=hp) + jnp.einsum(
        "ab,kbc->kac", sin_table, real_part, precision=hp
    )
    return (real_out, imag_out)


def right_product(real_part, imag_part, cos_table, sin_table):
    hp = lax.Precision.HIGHEST
    real_out = jnp.einsum("kab,bc->kac", real_part, cos_table, precision=hp) - jnp.einsum(
        "kab,bc->kac", imag_part, sin_table, precision=hp
    )
    imag_out = jnp.einsum("kab,bc->kac", real_part, sin_table, precision=hp) + jnp.einsum(
        "kab,bc->kac", imag_part, cos_table, precision=hp
    )
    return (real_out, imag_out)


def transform(real_part, imag_part, cos_table, sin_table):
    middle_re, middle_im = left_product(cos_table, sin_table, real_part, imag_part)
    return right_product(middle_re, middle_im, cos_table, sin_table)


def slot_terms(window, probe, pattern, cos_table, sin_table):
    window_re, window_im = (window[0], window[1])
    probe_re, probe_im = (probe[:, 0], probe[:, 1])
    exit_re = probe_re * window_re - probe_im * window_im
    exit_im = probe_re * window_im + probe_im * window_re
    far_re, far_im = transform(exit_re, exit_im, cos_table, sin_table)
    intensity = jnp.sum(far_re * far_re + far_im * far_im, axis=0)
    misfit = intensity - pattern
    back_re, back_im = transform(misfit * far_re, misfit * far_im, cos_table, -sin_table)
    grad_re = jnp.sum(probe_re * back_re + probe_im * back_im, axis=0)
    grad_im = jnp.sum(probe_re * back_im - probe_im * back_re, axis=0)
    term_re = window_re * back_re + window_im * back_im
    term_im = window_re * back_im - window_im * back_re
    return (jnp.stack([grad_re, grad_im]), jnp.stack([term_re, term_im], axis=1))


def body(object_field, probe, patterns, offsets, counts):
    width = probe.shape[-1]
    block = object_field.shape[1]
    slot_total = patterns.shape[2]
    cos_table, sin_table = dft_tables(width)
    tile_total = lax.axis_size("row") * lax.axis_size("col")
    live_count = counts[0, 0]
    frame = with_halo(object_field, (("row", 1), ("col", 2)), H)

    def slot_step(slot_index, inner):
        local_grad, probe_acc = inner
        slot_index = as_index(slot_index)
        corner_y = as_index(offsets[0, 0, slot_index, 0])
        corner_x = as_index(offsets[0, 0, slot_index, 1])
        window = lax.dynamic_slice(frame, (as_index(0), corner_y, corner_x), (2, width, width))
        window_grad, probe_term = slot_terms(
            window, probe, patterns[0, 0, slot_index], cos_table, sin_table
        )
        live = (slot_index < live_count).astype(jnp.float32)
        region = (
            lax.dynamic_slice(local_grad, (as_index(0), corner_y, corner_x), (2, width, width))
            + live * window_grad
        )
        local_grad = lax.dynamic_update_slice(local_grad, region, (as_index(0), corner_y, corner_x))
        return (local_grad, probe_acc + live * probe_term)

    start_carry = (jnp.zeros_like(frame), jnp.zeros_like(probe))
    gradient, probe_grad = lax.fori_loop(0, slot_total, slot_step, start_carry)
    upper_strip = gradient[:, :H, :]
    lower_strip = gradient[:, H + block :, :]
    middle = gradient[:, H : H + block, :]
    row_edges = jnp.concatenate([upper_strip, lower_strip], axis=1)
    row_grown = with_halo(row_edges, (("row", 1),), H)
    from_above = row_grown[:, :H, :]
    from_below = row_grown[:, 3 * H :, :]
    middle = middle.at[:, :H, :].add(from_above).at[:, block - H :, :].add(from_below)
    left_strip = middle[:, :, :H]
    right_strip = middle[:, :, H + block :]
    object_grad = middle[:, :, H : H + block]
    col_edges = jnp.concatenate([left_strip, right_strip], axis=2)
    col_grown = with_halo(col_edges, (("col", 2),), H)
    from_left = col_grown[:, :, :H]
    from_right = col_grown[:, :, 3 * H :]
    object_grad = object_grad.at[:, :, :H].add(from_left).at[:, :, block - H :].add(from_right)
    weight = (
        jnp.max(jnp.sum(probe[:, 0] * probe[:, 0] + probe[:, 1] * probe[:, 1], axis=0)) + epsilon
    )
    object_field = object_field - object_rate * object_grad / weight
    summed = lax.psum(probe_grad, ("row", "col"))
    probe = probe - probe_rate * summed / tile_total
    return (object_field, probe)


def solution(mesh):
    placed = (
        P(None, ("tilt", "row"), "col"),
        P("tilt", None, None, None),
        P(("tilt", "row"), "col", None, None, None),
        P(("tilt", "row"), "col", None, None),
        P(("tilt", "row"), "col"),
    )
    return jax.shard_map(
        body,
        mesh=mesh,
        in_specs=placed,
        out_specs=(P(None, ("tilt", "row"), "col"), P("tilt", None, None, None)),
        check_vma=False,
    )
```

profile of v0, /device:TPU:0, one launch (start us, length us, event | category | flops | bytes accessed | tf_op | source)
XLA Modules:
  0.0 179.6 jit_solution(4061278362378386647)
XLA Ops:
  7.2 4.9 %collective-permute-start = (f32[2,128,128]{2,1,0:T(8,128)}, f32[2,128,128]{2,1,0:T(8,128)S(1)}, u32[]{:S(2)}, u32[]{:S(2)}) collective-permute-start(f32[2,128,128]{2,1,0:T(8,128)} %param.23), channel_id=1, source_target_pairs={{0,2},{2,4},{4,6},{6,8},{8,10},{10,12},{12,14},{1,3},{3,5},{5,7},{... | collective-permute-start | bytes 393224 | tf_op jit(solution)/shard_map/ppermute | solution.py:17
  12.1 1.3 collective-permute-start.1
  13.4 1.7 collective-permute-done
  15.2 0.9 constant_dynamic-update-slice_fusion.1
  16.1 3.1 %collective-permute-done.1 = f32[2,128,128]{2,1,0:T(8,128)S(1)} collective-permute-done((f32[2,128,128]{2,1,0:T(8,128)}, f32[2,128,128]{2,1,0:T(8,128)S(1)}, u32[]{:S(2)}, u32[]{:S(2)}) %collective-permute-start.1) | collective-permute-done | bytes 131104 | tf_op jit(solution)/shard_map/ppermute | solution.py:20
  19.2 1.3 collective-permute-start.2
  20.5 1.3 collective-permute-start.3
  21.8 1.1 copy.41
  22.9 1.2 collective-permute-done.3
  24.1 1.1 pad_maximum_fusion
  25.3 0.8 copy-done.1
  26.1 42.0 %while.26 = (s32[]{:T(128)}, f32[2,384,384]{2,1,0:T(8,128)S(1)}, f32[4,2,128,128]{3,2,0,1:T(8,128)S(1)}, s32[1,1,2,2]{3,2,1,0:T(2,128)S(1)}, s32[]{:T(128)}, /*i...) while((s32[]{:T(128)}, f32[2,384,384]{2,1,0:T(8,128)S(1)}, ...), condition=%wide.region_4.5_spmd.clone.clone, body=%wide.region_0.4_spmd.clone.clone.sunk | while | flops 1617952768 | bytes 16646421 | solution.py:107
  30.7 1.1 dynamic-slice_bitcast_fusion.3
  44.8 2.2 %dynamic_update_slice.11 = f32[2,384,384]{2,1,0:T(8,128)S(1)} dynamic-update-slice(f32[2,384,384]{2,1,0:T(8,128)S(1)} %get-tuple-element.543, f32[2,128,128]{2,1,0:T(8,128)S(1)} %fusion.247, s32[]{:T(128)} %constant.191.clone.1..sunk, s32[]{:T(128)S(6)} %select_n.177, s32[]{:T(128)S(6)} %select_n.178) | dynamic-update-slice | bytes 262148 | tf_op jit(solution)/shard_map/while/body/eval_jaxpr/dynamic_update_slice | solution.py:103
  51.6 1.1 dynamic-slice_bitcast_fusion.3
  65.6 2.5 %dynamic_update_slice.11 = f32[2,384,384]{2,1,0:T(8,128)S(1)} dynamic-update-slice(f32[2,384,384]{2,1,0:T(8,128)S(1)} %get-tuple-element.543, f32[2,128,128]{2,1,0:T(8,128)S(1)} %fusion.247, s32[]{:T(128)} %constant.191.clone.1..sunk, s32[]{:T(128)S(6)} %select_n.177, s32[]{:T(128)S(6)} %select_n.178) | dynamic-update-slice | bytes 262148 | tf_op jit(solution)/shard_map/while/body/eval_jaxpr/dynamic_update_slice | solution.py:103
  69.0 4.5 %collective-permute-start.4 = (f32[2,128,384]{2,1,0:T(8,128)}, f32[2,128,384]{2,1,0:T(8,128)S(1)}, u32[]{:S(2)}, u32[]{:S(2)}) collective-permute-start(f32[2,128,384]{2,1,0:T(8,128)} %get-tuple-element.457), channel_id=1, source_target_pairs={{0,2},{2,4},{4,6},{6,8},{8,10},{10,12},{12,14},{1,3},{3,5},{5,7},{... | collective-permute-start | bytes 1179656 | tf_op jit(solution)/shard_map/ppermute | solution.py:17
  73.5 1.3 collective-permute-start.5
  76.1 0.8 copy.42
  77.0 14.1 %collective-permute-done.4 = f32[2,128,384]{2,1,0:T(8,128)S(1)} collective-permute-done((f32[2,128,384]{2,1,0:T(8,128)}, f32[2,128,384]{2,1,0:T(8,128)S(1)}, u32[]{:S(2)}, u32[]{:S(2)}) %collective-permute-start.4) | collective-permute-done | bytes 393248 | tf_op jit(solution)/shard_map/ppermute | solution.py:17
  91.1 1.4 collective-permute-start.6
  92.6 1.3 collective-permute-start.7
  93.9 76.3 %all-reduce.2.cloned.1.call-done = f32[4,2,128,128]{3,2,1,0:T(8,128)} async-done(((f32[4,2,128,128]{3,2,1,0:T(8,128)}), f32[4,2,128,128]{3,2,1,0:T(8,128)}) %all-reduce.2.cloned.1.call-update) | async-done | bytes 524304 | tf_op jit(solution)/shard_map/psum | solution.py:128
  170.2 1.9 %multiply_subtract_fusion = f32[4,2,128,128]{3,2,1,0:T(8,128)} fusion(f32[4,2,128,128]{3,2,1,0:T(8,128)S(1)} %copy-done, f32[4,2,128,128]{3,2,1,0:T(8,128)} %all-reduce.2.cloned.1.call-done), kind=kLoop, calls=%fused_computation.169 | loop fusion | flops 262144 | bytes 1572864 | tf_op jit(solution)/shard_map/sub | solution.py:129
  (63 shorter events, 28.0 us)
Async XLA Ops:
  7.2 163.0 %all-reduce.2.cloned.1.call-start = ((), (), s32[]{:S(2)}) async-start(), calls=%async_computation | async-start | bytes 1048576 | tf_op jit(solution)/shard_map/psum | solution.py:128
  7.2 7.9 %collective-permute-start = (f32[2,128,128]{2,1,0:T(8,128)}, f32[2,128,128]{2,1,0:T(8,128)S(1)}, u32[]{:S(2)}, u32[]{:S(2)}) collective-permute-start(f32[2,128,128]{2,1,0:T(8,128)} %param.23), channel_id=1, source_target_pairs={{0,2},{2,4},{4,6},{6,8},{8,10},{10,12},{12,14},{1,3},{3,5},{5,7},{... | collective-permute-start | bytes 393224 | tf_op jit(solution)/shard_map/ppermute | solution.py:17
  12.1 7.1 %collective-permute-start.1 = (f32[2,128,128]{2,1,0:T(8,128)}, f32[2,128,128]{2,1,0:T(8,128)S(1)}, u32[]{:S(2)}, u32[]{:S(2)}) collective-permute-start(f32[2,128,128]{2,1,0:T(8,128)} %param.23), channel_id=1, source_target_pairs={{2,0},{4,2},{6,4},{8,6},{10,8},{12,10},{14,12},{3,1},{5,3},{7,5},{... | collective-permute-start | bytes 393224 | tf_op jit(solution)/shard_map/ppermute | solution.py:20
  19.2 3.7 %collective-permute-start.2 = (f32[2,384,128]{2,1,0:T(8,128)S(1)}, f32[2,384,128]{2,1,0:T(8,128)S(1)}, u32[]{:S(2)}, u32[]{:S(2)}) collective-permute-start(f32[2,384,128]{2,1,0:T(8,128)S(1)} %constant_dynamic-update-slice_fusion), channel_id=1, source_target_pairs={{0,1},{2,3},{4,5},{6,7},{8,9},{10,11},{12,13},{14,15},{16,17},{18,... | collective-permute-start | bytes 1179656 | tf_op jit(solution)/shard_map/ppermute | solution.py:17
  20.5 3.6 %collective-permute-start.3 = (f32[2,384,128]{2,1,0:T(8,128)S(1)}, f32[2,384,128]{2,1,0:T(8,128)S(1)}, u32[]{:S(2)}, u32[]{:S(2)}) collective-permute-start(f32[2,384,128]{2,1,0:T(8,128)S(1)} %constant_dynamic-update-slice_fusion), channel_id=1, source_target_pairs={{1,0},{3,2},{5,4},{7,6},{9,8},{11,10},{13,12},{15,14},{17,16},{19,... | collective-permute-start | bytes 1179656 | tf_op jit(solution)/shard_map/ppermute | solution.py:20
  25.2 0.9 copy-start.1
  25.2 0.9 copy-start.3
  68.2 6.6 %copy-start = (f32[4,2,128,128]{3,2,1,0:T(8,128)S(1)}, f32[4,2,128,128]{3,2,1,0:T(8,128)}, u32[]{:S(2)}) copy-start(f32[4,2,128,128]{3,2,1,0:T(8,128)} %param.24) | copy-start | bytes 1572868
  69.0 22.0 %collective-permute-start.4 = (f32[2,128,384]{2,1,0:T(8,128)}, f32[2,128,384]{2,1,0:T(8,128)S(1)}, u32[]{:S(2)}, u32[]{:S(2)}) collective-permute-start(f32[2,128,384]{2,1,0:T(8,128)} %get-tuple-element.457), channel_id=1, source_target_pairs={{0,2},{2,4},{4,6},{6,8},{8,10},{10,12},{12,14},{1,3},{3,5},{5,7},{... | collective-permute-start | bytes 1179656 | tf_op jit(solution)/shard_map/ppermute | solution.py:17
  73.5 17.5 %collective-permute-start.5 = (f32[2,128,384]{2,1,0:T(8,128)S(1)}, f32[2,128,384]{2,1,0:T(8,128)S(1)}, u32[]{:S(2)}, u32[]{:S(2)}) collective-permute-start(f32[2,128,384]{2,1,0:T(8,128)S(1)} %get-tuple-element.458), channel_id=1, source_target_pairs={{2,0},{4,2},{6,4},{8,6},{10,8},{12,10},{14,12},{3,1},{5,3},{7,5},{... | collective-permute-start | bytes 1179656 | tf_op jit(solution)/shard_map/ppermute | solution.py:20
  91.1 81.0 %copy-start.2 = (f32[2,128,128]{2,1,0:T(8,128)S(1)}, f32[2,128,128]{2,1,0:T(8,128)}, u32[]{:S(2)}) copy-start(f32[2,128,128]{2,1,0:T(8,128)} %param.23) | copy-start | bytes 393220
  91.1 81.0 %collective-permute-start.6 = (f32[2,128,128]{2,1,0:T(8,128)S(1)}, f32[2,128,128]{2,1,0:T(8,128)S(1)}, u32[]{:S(2)}, u32[]{:S(2)}) collective-permute-start(f32[2,128,128]{2,1,0:T(8,128)S(1)} %get-tuple-element.459), channel_id=1, source_target_pairs={{0,1},{2,3},{4,5},{6,7},{8,9},{10,11},{12,13},{14,15},{16,17},{18,... | collective-permute-start | bytes 393224 | tf_op jit(solution)/shard_map/ppermute | solution.py:17
  92.6 79.5 %collective-permute-start.7 = (f32[2,128,128]{2,1,0:T(8,128)S(1)}, f32[2,128,128]{2,1,0:T(8,128)S(1)}, u32[]{:S(2)}, u32[]{:S(2)}) collective-permute-start(f32[2,128,128]{2,1,0:T(8,128)S(1)} %get-tuple-element.460), channel_id=1, source_target_pairs={{1,0},{3,2},{5,4},{7,6},{9,8},{11,10},{13,12},{15,14},{17,16},{19,... | collective-permute-start | bytes 393224 | tf_op jit(solution)/shard_map/ppermute | solution.py:20
Sparse Core Ops, SparseCore 0:
  77.1 93.0 all-reduce.1
where the time goes:
time: 180 us
  waiting for transfers between devices  96.5 us (54%)
  matrix products  23.8 us (13%)
  starting transfers between devices  17.3 us (10%)
  between operations  14.8 us (8%)
  local copies, waits for them, and re-layouts  12.6 us (7%)
  loops' own time  9.63 us (5%)
  other arithmetic  4.97 us (3%)
    psum x1, waiting for transfers between devices, body(): summed = lax.psum(probe_grad, ('row', 'col'))  76.3 us
    ppermute x4, waiting for transfers between devices, with_halo(): lax.ppermute(lax.slice_in_dim(block, block.shape[dim] - width, None, axis...  15.8 us
    ppermute x4, starting transfers between devices, with_halo(): lax.ppermute(lax.slice_in_dim(block, block.shape[dim] - width, None, axis...  12.1 us
    another operation x1, loops' own time, body(): gradient, probe_grad = lax.fori_loop(0, slot_total, slot_step, start_carry)  9.63 us
    ppermute x4, starting transfers between devices, with_halo(): lax.ppermute(lax.slice_in_dim(block, 0, width, axis=dim), axis, backward)  5.17 us
    dynamic_update_slice x2, local copies, waits for them, and re-layouts, slot_step(): lax.dynamic_update_slice(local_grad, region, (as_index(0), corner_y, corn...  4.66 us
    ppermute x4, waiting for transfers between devices, with_halo(): lax.ppermute(lax.slice_in_dim(block, 0, width, axis=dim), axis, backward)  4.31 us
  transfers between devices with their start and end apart: 9, of which 5 were waited for; matrix products, arithmetic and copies ran while one was open for 3% of the time, Pallas kernels for 0%

commit v1 on v0

--- a/solution.py
+++ b/solution.py
@@ -1,3 +1,4 @@
+import functools
 import jax
 import jax.numpy as jnp
 from jax import lax
@@ -7,6 +8,13 @@
 object_rate = 1.0
 probe_rate = 1.0
 epsilon = 1e-06
+
+
+def order_limits_now(xx, mesh_ax, named_axis):
+    return jax.lax.psum(jax.lax.psum(xx, mesh_ax), named_axis)
+
+
+open_classes_here = functools.partial(order_limits_now, mesh_ax="col", named_axis="row")
 
 
 def with_halo(block, sides, width):
@@ -125,7 +133,7 @@
         jnp.max(jnp.sum(probe[:, 0] * probe[:, 0] + probe[:, 1] * probe[:, 1], axis=0)) + epsilon
     )
     object_field = object_field - object_rate * object_grad / weight
-    summed = lax.psum(probe_grad, ("row", "col"))
+    summed = open_classes_here(probe_grad)
     probe = probe - probe_rate * summed / tile_total
     return (object_field, probe)
 

time: 180 us -> 182 us (1.011)
  waiting for transfers between devices: 96.5 us -> 98.4 us
    psum x1 -> x2, waiting for transfers between devices: 76.3 us -> 77.6 us  [order_limits_now(): return jax.lax.psum(jax.lax.psum(xx, mesh_ax), named_axis)]
  transfers between devices with their start and end apart: 9 -> 10, of which waited for: 5 -> 7; matrix products, arithmetic and copies ran while one was open for 3% -> 2% of each run, Pallas kernels for 0% -> 0%
where the time goes in v1:
time: 182 us
  waiting for transfers between devices  98.4 us (54%)
  matrix products  23.8 us (13%)
  starting transfers between devices  18.1 us (10%)
  between operations  14.9 us (8%)
  local copies, waits for them, and re-layouts  11.9 us (7%)
  loops' own time  9.63 us (5%)
  other arithmetic  4.96 us (3%)
    psum x2, waiting for transfers between devices, order_limits_now(): return jax.lax.psum(jax.lax.psum(xx, mesh_ax), named_axis)  77.6 us
    ppermute x4, waiting for transfers between devices, with_halo(): lax.ppermute(lax.slice_in_dim(block, block.shape[dim] - width, None, axis...  15.8 us
    ppermute x4, starting transfers between devices, with_halo(): lax.ppermute(lax.slice_in_dim(block, block.shape[dim] - width, None, axis...  12.9 us
    another operation x1, loops' own time, body(): gradient, probe_grad = lax.fori_loop(0, slot_total, slot_step, start_carry)  9.63 us
    ppermute x4, starting transfers between devices, with_halo(): lax.ppermute(lax.slice_in_dim(block, 0, width, axis=dim), axis, backward)  5.17 us
    ppermute x4, waiting for transfers between devices, with_halo(): lax.ppermute(lax.slice_in_dim(block, 0, width, axis=dim), axis, backward)  4.92 us
    dynamic_update_slice x2, local copies, waits for them, and re-layouts, slot_step(): lax.dynamic_update_slice(local_grad, region, (as_index(0), corner_y, corn...  4.66 us
  transfers between devices with their start and end apart: 10, of which 7 were waited for; matrix products, arithmetic and copies ran while one was open for 2% of the time, Pallas kernels for 0%

profile of v1, /device:TPU:0, one launch (start us, length us, event | category | flops | bytes accessed | tf_op | source)
XLA Modules:
  0.0 181.6 jit_solution(8756795640430662466)
XLA Ops:
  7.2 4.9 %collective-permute-start = (f32[2,128,128]{2,1,0:T(8,128)}, f32[2,128,128]{2,1,0:T(8,128)S(1)}, u32[]{:S(2)}, u32[]{:S(2)}) collective-permute-start(f32[2,128,128]{2,1,0:T(8,128)} %param.23), channel_id=1, source_target_pairs={{0,2},{2,4},{4,6},{6,8},{8,10},{10,12},{12,14},{1,3},{3,5},{5,7},{... | collective-permute-start | bytes 393224 | tf_op jit(solution)/shard_map/ppermute | solution.py:25
  12.1 1.3 collective-permute-start.1
  13.4 1.7 collective-permute-done
  15.2 0.9 constant_dynamic-update-slice_fusion.1
  16.1 3.1 %collective-permute-done.1 = f32[2,128,128]{2,1,0:T(8,128)S(1)} collective-permute-done((f32[2,128,128]{2,1,0:T(8,128)}, f32[2,128,128]{2,1,0:T(8,128)S(1)}, u32[]{:S(2)}, u32[]{:S(2)}) %collective-permute-start.1) | collective-permute-done | bytes 131104 | tf_op jit(solution)/shard_map/ppermute | solution.py:28
  19.2 1.3 collective-permute-start.2
  20.5 1.3 collective-permute-start.3
  21.8 1.1 copy.41
  22.9 1.2 collective-permute-done.3
  24.1 1.1 pad_maximum_fusion
  26.1 42.0 %while.26 = (s32[]{:T(128)}, f32[2,384,384]{2,1,0:T(8,128)S(1)}, f32[4,2,128,128]{3,2,0,1:T(8,128)S(1)}, s32[1,1,2,2]{3,2,1,0:T(2,128)S(1)}, s32[]{:T(128)}, /*i...) while((s32[]{:T(128)}, f32[2,384,384]{2,1,0:T(8,128)S(1)}, ...), condition=%wide.region_4.5_spmd.clone.clone, body=%wide.region_0.4_spmd.clone.clone.sunk | while | flops 1617952768 | bytes 16646421 | solution.py:115
  30.7 1.1 dynamic-slice_bitcast_fusion.3
  44.8 2.2 %dynamic_update_slice.11 = f32[2,384,384]{2,1,0:T(8,128)S(1)} dynamic-update-slice(f32[2,384,384]{2,1,0:T(8,128)S(1)} %get-tuple-element.543, f32[2,128,128]{2,1,0:T(8,128)S(1)} %fusion.247, s32[]{:T(128)} %constant.191.clone.1..sunk, s32[]{:T(128)S(6)} %select_n.177, s32[]{:T(128)S(6)} %select_n.178) | dynamic-update-slice | bytes 262148 | tf_op jit(solution)/shard_map/while/body/eval_jaxpr/dynamic_update_slice | solution.py:111
  51.6 1.1 dynamic-slice_bitcast_fusion.3
  65.6 2.5 %dynamic_update_slice.11 = f32[2,384,384]{2,1,0:T(8,128)S(1)} dynamic-update-slice(f32[2,384,384]{2,1,0:T(8,128)S(1)} %get-tuple-element.543, f32[2,128,128]{2,1,0:T(8,128)S(1)} %fusion.247, s32[]{:T(128)} %constant.191.clone.1..sunk, s32[]{:T(128)S(6)} %select_n.177, s32[]{:T(128)S(6)} %select_n.178) | dynamic-update-slice | bytes 262148 | tf_op jit(solution)/shard_map/while/body/eval_jaxpr/dynamic_update_slice | solution.py:111
  68.2 4.5 %collective-permute-start.4 = (f32[2,128,384]{2,1,0:T(8,128)S(1)}, f32[2,128,384]{2,1,0:T(8,128)S(1)}, u32[]{:S(2)}, u32[]{:S(2)}) collective-permute-start(f32[2,128,384]{2,1,0:T(8,128)S(1)} %get-tuple-element.457), channel_id=1, source_target_pairs={{0,2},{2,4},{4,6},{6,8},{8,10},{10,12},{12,14},{1,3},{3,5},{5,7},{... | collective-permute-start | bytes 1179656 | tf_op jit(solution)/shard_map/ppermute | solution.py:25
  72.8 1.3 collective-permute-start.5
  74.1 0.8 copy.42
  75.0 14.1 %collective-permute-done.4 = f32[2,128,384]{2,1,0:T(8,128)S(1)} collective-permute-done((f32[2,128,384]{2,1,0:T(8,128)S(1)}, f32[2,128,384]{2,1,0:T(8,128)S(1)}, u32[]{:S(2)}, u32[]{:S(2)}) %collective-permute-start.4) | collective-permute-done | bytes 393248 | tf_op jit(solution)/shard_map/ppermute | solution.py:25
  89.1 6.4 %all-reduce.3.cloned.1.call-done = f32[4,2,128,128]{3,2,1,0:T(8,128)} async-done(((f32[4,2,128,128]{3,2,1,0:T(8,128)}), f32[4,2,128,128]{3,2,1,0:T(8,128)}) %all-reduce.3.cloned.1.call-update) | async-done | bytes 524304 | tf_op jit(solution)/shard_map/psum | solution.py:14
  95.6 2.2 %collective-permute-start.6 = (f32[2,128,128]{2,1,0:T(8,128)S(1)}, f32[2,128,128]{2,1,0:T(8,128)S(1)}, u32[]{:S(2)}, u32[]{:S(2)}) collective-permute-start(f32[2,128,128]{2,1,0:T(8,128)S(1)} %get-tuple-element.459), channel_id=1, source_target_pairs={{0,1},{2,3},{4,5},{6,7},{8,9},{10,11},{12,13},{14,15},{16,17},{18,... | collective-permute-start | bytes 393224 | tf_op jit(solution)/shard_map/ppermute | solution.py:25
  97.8 1.3 collective-permute-start.7
  101.7 71.2 %all-reduce.5.cloned.1.call-done = f32[4,2,128,128]{3,2,1,0:T(8,128)} async-done(((f32[4,2,128,128]{3,2,1,0:T(8,128)}), f32[4,2,128,128]{3,2,1,0:T(8,128)}) %all-reduce.5.cloned.1.call-update) | async-done | bytes 524304 | tf_op jit(solution)/shard_map/psum | solution.py:14
  172.9 1.9 %multiply_subtract_fusion = f32[4,2,128,128]{3,2,1,0:T(8,128)} fusion(f32[4,2,128,128]{3,2,1,0:T(8,128)S(1)} %copy-done, f32[4,2,128,128]{3,2,1,0:T(8,128)} %all-reduce.5.cloned.1.call-done), kind=kLoop, calls=%fused_computation.169 | loop fusion | flops 262144 | bytes 1572864 | tf_op jit(solution)/shard_map/sub | solution.py:137
  (66 shorter events, 28.7 us)
Async XLA Ops:
  7.2 88.4 %all-reduce.3.cloned.1.call-start = ((), (), s32[]{:S(2)}) async-start(), calls=%async_computation | async-start | bytes 1048576 | tf_op jit(solution)/shard_map/psum | solution.py:14
  7.2 7.9 %collective-permute-start = (f32[2,128,128]{2,1,0:T(8,128)}, f32[2,128,128]{2,1,0:T(8,128)S(1)}, u32[]{:S(2)}, u32[]{:S(2)}) collective-permute-start(f32[2,128,128]{2,1,0:T(8,128)} %param.23), channel_id=1, source_target_pairs={{0,2},{2,4},{4,6},{6,8},{8,10},{10,12},{12,14},{1,3},{3,5},{5,7},{... | collective-permute-start | bytes 393224 | tf_op jit(solution)/shard_map/ppermute | solution.py:25
  12.1 7.1 %collective-permute-start.1 = (f32[2,128,128]{2,1,0:T(8,128)}, f32[2,128,128]{2,1,0:T(8,128)S(1)}, u32[]{:S(2)}, u32[]{:S(2)}) collective-permute-start(f32[2,128,128]{2,1,0:T(8,128)} %param.23), channel_id=1, source_target_pairs={{2,0},{4,2},{6,4},{8,6},{10,8},{12,10},{14,12},{3,1},{5,3},{7,5},{... | collective-permute-start | bytes 393224 | tf_op jit(solution)/shard_map/ppermute | solution.py:28
  19.2 3.7 %collective-permute-start.2 = (f32[2,384,128]{2,1,0:T(8,128)S(1)}, f32[2,384,128]{2,1,0:T(8,128)S(1)}, u32[]{:S(2)}, u32[]{:S(2)}) collective-permute-start(f32[2,384,128]{2,1,0:T(8,128)S(1)} %constant_dynamic-update-slice_fusion), channel_id=1, source_target_pairs={{0,1},{2,3},{4,5},{6,7},{8,9},{10,11},{12,13},{14,15},{16,17},{18,... | collective-permute-start | bytes 1179656 | tf_op jit(solution)/shard_map/ppermute | solution.py:25
  20.5 3.6 %collective-permute-start.3 = (f32[2,384,128]{2,1,0:T(8,128)S(1)}, f32[2,384,128]{2,1,0:T(8,128)S(1)}, u32[]{:S(2)}, u32[]{:S(2)}) collective-permute-start(f32[2,384,128]{2,1,0:T(8,128)S(1)} %constant_dynamic-update-slice_fusion), channel_id=1, source_target_pairs={{1,0},{3,2},{5,4},{7,6},{9,8},{11,10},{13,12},{15,14},{17,16},{19,... | collective-permute-start | bytes 1179656 | tf_op jit(solution)/shard_map/ppermute | solution.py:28
  25.2 0.9 copy-start.1
  25.2 0.9 copy-start.3
  68.2 20.8 %collective-permute-start.4 = (f32[2,128,384]{2,1,0:T(8,128)S(1)}, f32[2,128,384]{2,1,0:T(8,128)S(1)}, u32[]{:S(2)}, u32[]{:S(2)}) collective-permute-start(f32[2,128,384]{2,1,0:T(8,128)S(1)} %get-tuple-element.457), channel_id=1, source_target_pairs={{0,2},{2,4},{4,6},{6,8},{8,10},{10,12},{12,14},{1,3},{3,5},{5,7},{... | collective-permute-start | bytes 1179656 | tf_op jit(solution)/shard_map/ppermute | solution.py:25
  72.8 16.3 %collective-permute-start.5 = (f32[2,128,384]{2,1,0:T(8,128)S(1)}, f32[2,128,384]{2,1,0:T(8,128)S(1)}, u32[]{:S(2)}, u32[]{:S(2)}) collective-permute-start(f32[2,128,384]{2,1,0:T(8,128)S(1)} %get-tuple-element.458), channel_id=1, source_target_pairs={{2,0},{4,2},{6,4},{8,6},{10,8},{12,10},{14,12},{3,1},{5,3},{7,5},{... | collective-permute-start | bytes 1179656 | tf_op jit(solution)/shard_map/ppermute | solution.py:28
  74.9 24.2 %copy-start = (f32[4,2,128,128]{3,2,1,0:T(8,128)S(1)}, f32[4,2,128,128]{3,2,1,0:T(8,128)}, u32[]{:S(2)}) copy-start(f32[4,2,128,128]{3,2,1,0:T(8,128)} %param.24) | copy-start | bytes 1572868
  74.9 98.0 %all-reduce.5.cloned.1.call-start = ((), (), s32[]{:S(2)}) async-start(), calls=%async_computation.1 | async-start | bytes 1048576 | tf_op jit(solution)/shard_map/psum | solution.py:14
  89.1 11.9 %copy-start.2 = (f32[2,128,128]{2,1,0:T(8,128)S(1)}, f32[2,128,128]{2,1,0:T(8,128)}, u32[]{:S(2)}) copy-start(f32[2,128,128]{2,1,0:T(8,128)} %param.23) | copy-start | bytes 393220
  95.6 4.8 %collective-permute-start.6 = (f32[2,128,128]{2,1,0:T(8,128)S(1)}, f32[2,128,128]{2,1,0:T(8,128)S(1)}, u32[]{:S(2)}, u32[]{:S(2)}) collective-permute-start(f32[2,128,128]{2,1,0:T(8,128)S(1)} %get-tuple-element.459), channel_id=1, source_target_pairs={{0,1},{2,3},{4,5},{6,7},{8,9},{10,11},{12,13},{14,15},{16,17},{18,... | collective-permute-start | bytes 393224 | tf_op jit(solution)/shard_map/ppermute | solution.py:25
  97.8 3.2 %collective-permute-start.7 = (f32[2,128,128]{2,1,0:T(8,128)S(1)}, f32[2,128,128]{2,1,0:T(8,128)S(1)}, u32[]{:S(2)}, u32[]{:S(2)}) collective-permute-start(f32[2,128,128]{2,1,0:T(8,128)S(1)} %get-tuple-element.460), channel_id=1, source_target_pairs={{1,0},{3,2},{5,4},{7,6},{9,8},{11,10},{13,12},{15,14},{17,16},{19,... | collective-permute-start | bytes 393224 | tf_op jit(solution)/shard_map/ppermute | solution.py:28
Sparse Core Ops, SparseCore 0:
  75.0 20.4 all-reduce.2
  99.0 73.8 all-reduce.4
